TPU v7x, 512 devices: a whole 4x8x8 slice. The times are simulated.
512 devices in a mesh: gx: 16 (over y, core), gy: 8 (over z_hi, x), gz: 4 (over z_lo).
Axes of the slice: x: 4, y: 8, z: 8 (z_hi: 2, z_lo: 4; z = z_hi * 4 + z_lo), core: 2. Of those that a mesh axis runs over, the one named last changes fastest.
Arguments:
- positions: float32 [3, 16, 8, 4, 512], P(None, 'gx', 'gy', 'gz'), may hold values from 0 to 1
- velocities: float32 [3, 16, 8, 4, 512], P(None, 'gx', 'gy', 'gz'), may hold values from -6 to 6
- charges: float32 [16, 8, 4, 512], P('gx', 'gy', 'gz'), may hold values from -5 to 5
- cluster_atoms: int32 [16, 8, 4, 768], P('gx', 'gy', 'gz'), may hold values from 0 to 512, as said below
- pair_list: int32 [3, 16, 8, 4, 256], P(None, 'gx', 'gy', 'gz'), may hold values from 0 to 124, as said below
Outputs:
- new_positions: float32 [3, 16, 8, 4, 512], P(None, 'gx', 'gy', 'gz')
- new_velocities: float32 [3, 16, 8, 4, 512], P(None, 'gx', 'gy', 'gz')
- last_forces: float32 [3, 16, 8, 4, 512], P(None, 'gx', 'gy', 'gz')
Inputs may be any that keep to these rules, and one draw needn't show every extreme that they name: `cluster_atoms`: on every domain each atom index below 512 stands in exactly one slot; all other slots hold 512, meaning empty. `pair_list`: row 0 and row 1 lie in 0 to 5, row 2 in 0 to 124; on every domain each of the 125 shift indices appears in at least 2 listed pairs.
All inputs are finite; a program needn't handle non-finite values.
Results may differ from a plain program's by a relative error of at most 0.0001.
Values sent between devices are 32-bit elements; how exact they have to be, the bound alone decides.
A program may use at most 64 MiB of HBM per device.

v0:
```python
import functools

import jax
import jax.numpy as jnp
from jax import lax
from jax.experimental import pallas as pl
from jax.experimental.pallas import tpu as pltpu
from jax.sharding import PartitionSpec as P

CLUSTER = 128
STEPS = 2
TIME_STEP = 0.02
MESH = pl.DeviceIdType.MESH
AXES = ("gx", "gy", "gz")
VMEM = pl.BlockSpec(memory_space=pltpu.VMEM)
SMEM = pl.BlockSpec(memory_space=pltpu.SMEM)
UNROLL = 32


def split3(value):
    hi = value.astype(jnp.bfloat16)
    rest = value - hi.astype(jnp.float32)
    mid = rest.astype(jnp.bfloat16)
    lo = (rest - mid.astype(jnp.float32)).astype(jnp.bfloat16)
    return hi, mid, lo


class Zone:
    def __init__(self, sizes):
        self.sizes = sizes
        self.spans = tuple(min(5, n) for n in sizes)
        self.lows = tuple(-2 if n >= 5 else 0 for n in sizes)
        self.count = self.spans[0] * self.spans[1] * self.spans[2]
        own = tuple(-low for low in self.lows)
        self.paired = max(sizes) <= 4 and sizes[0] % 2 == 0
        self.plane = self.spans[1] * self.spans[2]
        self.own = (own[0] * self.spans[1] + own[1]) * self.spans[2] + own[2]

    def place(self, deltas):
        index = 0
        for delta, n, span in zip(deltas, self.sizes, self.spans):
            if n >= 5:
                here = delta + 2
            elif n in (1, 2, 4):
                here = (delta + 2 * n) & (n - 1)
            else:
                here = lax.rem(delta + 2 * n, n)
            index = index * span + here
        return index

    def peer(self, index, sign):
        parts = (
            index // (self.spans[1] * self.spans[2]),
            (index // self.spans[2]) % self.spans[1],
            index % self.spans[2],
        )
        out = []
        for axis, n, low, part in zip(AXES, self.sizes, self.lows, parts):
            out.append((lax.axis_index(axis) + sign * (part + low) + 2 * n) % n)
        return tuple(out)

    def turn(self):
        return 1 - 2 * (lax.axis_index(AXES[0]) % 2)

    def partner(self):
        return (lax.axis_index(AXES[0]) + self.turn(),) + tuple(
            lax.axis_index(axis) for axis in AXES[1:]
        )

    def seen_by_partner(self, index):
        return (index - self.turn() * self.plane + self.count) % self.count

    def alike(self, body):
        def step(k, carry):
            body((k // self.plane) * 2 * self.plane + k % self.plane)
            return carry

        lax.fori_loop(1, self.count // 2, step, 0)

    def others(self, body):
        def step(k, carry):
            body((self.own + 1 + k) % self.count)
            return carry

        lax.fori_loop(0, self.count - 1, step, 0)


def one_hot(atoms_ref, atom_count):
    slots = atoms_ref.shape[1]
    rows = lax.broadcasted_iota(jnp.int32, (atom_count, slots), 0)
    return jnp.where(rows == atoms_ref[...], 1.0, 0.0).astype(jnp.bfloat16)


def rows_where(count, index):
    rows = lax.broadcasted_iota(jnp.int32, (count, index.shape[1]), 0)
    return jnp.where(rows == index, 1.0, 0.0).astype(jnp.bfloat16)


def exact_dot(selector, values):
    return sum(
        jnp.dot(selector, piece, preferred_element_type=jnp.float32) for piece in split3(values)
    )


def side_by_side(ref):
    return jnp.concatenate([ref[c] for c in range(ref.shape[0])], axis=1)


def share(zone, src, dst_ref, send_sem, recv_sem):
    def copy(index):
        return pltpu.make_async_remote_copy(
            src_ref=src,
            dst_ref=dst_ref.at[index],
            send_sem=send_sem.at[index],
            recv_sem=recv_sem.at[index],
            device_id=zone.peer(index, -1),
            device_id_type=MESH,
        )

    if not zone.paired:
        zone.others(lambda index: copy(index).start())
        zone.others(lambda index: copy(index).wait())
        return

    def relay(index, block):
        place = zone.seen_by_partner(index)
        return pltpu.make_async_remote_copy(
            src_ref=block,
            dst_ref=dst_ref.at[place],
            send_sem=send_sem.at[(index + zone.plane) % zone.count],
            recv_sem=recv_sem.at[place],
            device_id=zone.partner(),
            device_id_type=MESH,
        )

    zone.alike(lambda index: copy(index).start())
    relay(zone.own, src).start()

    def pass_on(index):
        copy(index).wait_recv()
        relay(index, dst_ref.at[index]).start()

    zone.alike(pass_on)
    zone.alike(lambda index: copy(index).wait_send())

    def settle(k, carry):
        index = (k // zone.plane) * 2 * zone.plane + k % zone.plane
        relay(index, src).wait_send()
        arrived = pltpu.make_async_remote_copy(
            src_ref=src,
            dst_ref=dst_ref.at[index + zone.plane],
            send_sem=send_sem.at[index + zone.plane],
            recv_sem=recv_sem.at[index + zone.plane],
            device_id=zone.partner(),
            device_id_type=MESH,
        )
        arrived.wait_recv()
        return carry

    lax.fori_loop(0, zone.count // 2, settle, 0)


def gathered_force(zone, force_ref, land_ref, send_sem, recv_sem):
    def copy(index):
        return pltpu.make_async_remote_copy(
            src_ref=force_ref.at[index],
            dst_ref=land_ref.at[index],
            send_sem=send_sem.at[index],
            recv_sem=recv_sem.at[index],
            device_id=zone.peer(index, 1),
            device_id_type=MESH,
        )

    if not zone.paired:
        zone.others(lambda index: copy(index).start())
        zone.others(lambda index: copy(index).wait())

        def add(k, total):
            return total + land_ref[(zone.own + 1 + k) % zone.count]

        return lax.fori_loop(0, zone.count - 1, add, force_ref[zone.own])

    def handed(part):
        odd = (2 * part + 1) * zone.plane
        return pltpu.make_async_remote_copy(
            src_ref=force_ref.at[pl.ds(odd, zone.plane)],
            dst_ref=land_ref.at[pl.ds(zone.count + zone.seen_by_partner(odd), zone.plane)],
            send_sem=send_sem.at[odd],
            recv_sem=recv_sem.at[zone.count + zone.seen_by_partner(odd)],
            device_id=zone.partner(),
            device_id_type=MESH,
        )

    def taken(part):
        even = 2 * part * zone.plane
        return pltpu.make_async_remote_copy(
            src_ref=force_ref.at[pl.ds(even, zone.plane)],
            dst_ref=land_ref.at[pl.ds(zone.count + even, zone.plane)],
            send_sem=send_sem.at[even],
            recv_sem=recv_sem.at[zone.count + even],
            device_id=zone.partner(),
            device_id_type=MESH,
        )

    parts = zone.count // (2 * zone.plane)
    for part in range(parts):
        handed(part).start()
    for part in range(parts):
        taken(part).wait_recv()
        even = 2 * part * zone.plane
        for k in range(zone.plane):
            force_ref[even + k] += land_ref[zone.count + even + k]
    zone.alike(lambda index: copy(index).start())
    for part in range(parts):
        handed(part).wait_send()
    zone.alike(lambda index: copy(index).wait())

    def add(k, total):
        return total + land_ref[(k // zone.plane) * 2 * zone.plane + k % zone.plane]

    return lax.fori_loop(1, zone.count // 2, add, force_ref[zone.own])


def weighted(coords, charge):
    charge = 0.125 * charge
    part = jnp.concatenate([charge * c for c in coords] + [charge], axis=0)
    pieces = [p.astype(jnp.float32) for p in split3(part)]
    stacked = jnp.concatenate(pieces + [jnp.zeros_like(part)], axis=0).astype(jnp.bfloat16)
    return jnp.concatenate([stacked, stacked], axis=1)


def folded(out):
    return out[0:4] + out[4:8] + out[8:12]


def shift_of(t):
    t25 = (t * 5243) >> 17
    t5 = (t * 205) >> 10
    return t25 - 2, t5 - 5 * t25 - 2, t - 5 * t5 - 2


def pair_forces(zone, clusters, pairs_ref, x_ref, q_ref, force_ref, left_ref, lw_ref,
                f_ref, right_sum_ref, left_sum_ref, zone_hot_ref, home_hot_ref):
    own = zone.own
    for k in range(clusters):
        coords = []
        for c in range(3):
            row = x_ref[own, pl.ds(c * clusters + k, 1), :]
            coords.append(row)
            left_ref[k, c] = jnp.transpose(jnp.broadcast_to(0.5 * row, (CLUSTER, CLUSTER)))
        lw_ref[k] = weighted(coords, q_ref[own, pl.ds(3 * clusters + k, 1), :])

    def right_side(p):
        j = pairs_ref[1, 0, p]
        deltas = shift_of(pairs_ref[2, 0, p])
        z = zone.place(deltas)
        coords = [
            x_ref[z, pl.ds(c * clusters + j, 1), :] + deltas[c].astype(jnp.float32)
            for c in range(3)
        ]
        return coords, q_ref[z, pl.ds(3 * clusters + j, 1), :]

    def geometry(b, which=range(UNROLL)):
        for n in which:
            p = b * UNROLL + n
            coords, _ = right_side(p)
            i = pairs_ref[0, 0, p]
            r2 = None
            for c in range(3):
                d = left_ref[i, c] - 0.5 * coords[c]
                r2 = d * d if r2 is None else r2 + d * d
            g = jnp.maximum(1.0 - r2, 0.0)
            den = r2 + 0.125
            start = pl.reciprocal(den, approx=True)
            t = (g * start) * (2.0 - den * start)
            f = (g * t) * (t + 3.0)
            hi = f.astype(jnp.bfloat16)
            f_ref[n, 0] = hi
            f_ref[n, 1] = (f - hi.astype(jnp.float32)).astype(jnp.bfloat16)

    def sums(b, which=range(UNROLL)):
        found = []
        for n in which:
            p = b * UNROLL + n
            hi, lo = f_ref[n, 0], f_ref[n, 1]
            coords, charge = right_side(p)
            left = lax.dot_general(
                weighted(coords, charge), jnp.concatenate([hi, lo], axis=1),
                (((1,), (1,)), ((), ())), preferred_element_type=jnp.float32,
            )
            right = jnp.dot(
                lw_ref[pairs_ref[0, 0, p]], jnp.concatenate([hi, lo], axis=0),
                preferred_element_type=jnp.float32,
            )
            found.append((p, coords, charge, left, right))
        return found

    def keep(found):
        for p, coords, charge, left, right in found:
            left = folded(left)
            right = folded(right)
            for c in range(4):
                left_sum_ref[c, pl.ds(p, 1), :] = left[c : c + 1]
            for c in range(3):
                right_sum_ref[c, pl.ds(p, 1), :] = charge * (
                    coords[c] * right[3:4] - right[c : c + 1]
                )

    blocks = pairs_ref.shape[2] // UNROLL
    geometry(0)

    def block(b, carry):
        found = []
        for n in range(UNROLL):
            found += sums(b - 1, [n])
            geometry(b, [n])
            if n > 1:
                keep(found[n - 2 : n - 1])
        keep(found[-2:])
        return carry

    lax.fori_loop(1, blocks, block, 0)
    keep(sums(blocks - 1))

    zone_out = exact_dot(zone_hot_ref[...], side_by_side(right_sum_ref))
    home_out = exact_dot(home_hot_ref[...], side_by_side(left_sum_ref))
    for z in range(zone.count):
        for c in range(3):
            force_ref[z, c * clusters : (c + 1) * clusters, :] = zone_out[
                z * 8 : z * 8 + clusters, c * CLUSTER : (c + 1) * CLUSTER
            ]
    for c in range(3):
        rows = slice(c * clusters, (c + 1) * clusters)
        total = home_out[0:clusters, 3 * CLUSTER :]
        moment = home_out[0:clusters, c * CLUSTER : (c + 1) * CLUSTER]
        charge = q_ref[own, 3 * clusters : 4 * clusters, :]
        force_ref[own, rows, :] += charge * (x_ref[own, rows, :] * total - moment)


def kernel(zone, pairs_ref, pairs_vec_ref, x_in, v_in, q_in, atoms_ref, x_out, v_out, f_out,
           zone0_ref, zone1_ref, vel_ref, pos_ref, force_ref, land_ref, slot_ref, left_ref, lw_ref, f_ref,
           right_sum_ref, left_sum_ref, zone_hot_ref, home_hot_ref, send_sem, recv_sem):
    atom_count = x_in.shape[2]
    slots = atoms_ref.shape[1]
    clusters = slots // CLUSTER
    rows = 3 * clusters
    own = zone.own
    barrier = pltpu.get_barrier_semaphore()
    zone.others(lambda index: pl.semaphore_signal(
        barrier, 1, device_id=zone.peer(index, 1), device_id_type=MESH))

    data = jnp.concatenate(
        [x_in[c] for c in range(3)] + [v_in[c] for c in range(3)]
        + [q_in[...], jnp.zeros((1, atom_count), jnp.float32)], axis=0
    )
    hi, mid, lo = split3(data)
    stacked = jnp.concatenate([hi, mid, lo, jnp.zeros_like(hi)], axis=0)
    out = jnp.dot(stacked, one_hot(atoms_ref, atom_count), preferred_element_type=jnp.float32)
    slot = out[0:8] + out[8:16] + out[16:24]
    for k in range(clusters):
        lanes = slice(k * CLUSTER, (k + 1) * CLUSTER)
        for c in range(3):
            zone0_ref[own, c * clusters + k, :] = slot[c, lanes]
            vel_ref[c * clusters + k, :] = slot[3 + c, lanes]
        zone0_ref[own, 3 * clusters + k, :] = slot[6, lanes]
    deltas = shift_of(pairs_vec_ref[2])
    zone_hot_ref[...] = rows_where(zone.count * 8, zone.place(deltas) * 8 + pairs_vec_ref[1])
    home_hot_ref[...] = rows_where(8, pairs_vec_ref[0])
    pl.semaphore_wait(barrier, zone.count - 1)
    share(zone, zone0_ref.at[own], zone0_ref, send_sem.at[0], recv_sem.at[0])

    for step in range(STEPS):
        x_ref = zone0_ref if step == 0 else zone1_ref.at[step - 1]
        pair_forces(zone, clusters, pairs_ref, x_ref, zone0_ref, force_ref, left_ref, lw_ref,
                    f_ref, right_sum_ref, left_sum_ref, zone_hot_ref, home_hot_ref)
        force = gathered_force(zone, force_ref, land_ref.at[step],
                               send_sem.at[2 * step + 1], recv_sem.at[2 * step + 1])
        velocity = vel_ref[...] + TIME_STEP * force
        coords = x_ref[own, 0:rows, :] + TIME_STEP * velocity
        if step < STEPS - 1:
            vel_ref[...] = velocity
            zone1_ref[step, own] = coords
            share(zone, zone1_ref.at[step, own], zone1_ref.at[step],
                  send_sem.at[2 * step + 2], recv_sem.at[2 * step + 2])

    slot_ref[...] = jnp.zeros_like(slot_ref)
    for k in range(clusters):
        lanes = slice(k * CLUSTER, (k + 1) * CLUSTER)
        for c in range(3):
            r = c * clusters + k
            slot_ref[pl.ds(c, 1), lanes] = coords[r : r + 1]
            slot_ref[pl.ds(3 + c, 1), lanes] = velocity[r : r + 1]
            slot_ref[pl.ds(6 + c, 1), lanes] = force[r : r + 1]
    stacked = jnp.concatenate(split3(slot_ref[...]), axis=0)
    out = lax.dot_general(
        stacked, one_hot(atoms_ref, atom_count), (((1,), (1,)), ((), ())),
        preferred_element_type=jnp.float32,
    )
    atom = out[0:16] + out[16:32] + out[32:48]
    for c in range(3):
        x_out[c] = atom[c : c + 1]
        v_out[c] = atom[3 + c : 4 + c]
        f_out[c] = atom[6 + c : 7 + c]


def shards(sizes, positions, velocities, charges, cluster_atoms, pair_list):
    zone = Zone(sizes)
    atom_count = positions.shape[-1]
    slots = cluster_atoms.shape[-1]
    pair_count = pair_list.shape[-1]
    clusters = slots // CLUSTER
    rows = 3 * clusters
    f32, bf16 = jnp.float32, jnp.bfloat16
    x = positions.reshape(3, 1, atom_count)
    v = velocities.reshape(3, 1, atom_count)
    q = charges.reshape(1, atom_count)
    atoms = cluster_atoms.reshape(1, slots)
    pairs = pair_list.reshape(3, 1, pair_count)
    shape = jax.ShapeDtypeStruct((3, 1, atom_count), f32)
    outs = pl.pallas_call(
        functools.partial(kernel, zone),
        out_shape=(shape, shape, shape),
        in_specs=[SMEM] + [VMEM] * 5,
        out_specs=(VMEM, VMEM, VMEM),
        scratch_shapes=[
            pltpu.VMEM((zone.count, 4 * clusters, CLUSTER), f32),
            pltpu.VMEM((STEPS - 1, zone.count, rows, CLUSTER), f32),
            pltpu.VMEM((rows, CLUSTER), f32),
            pltpu.VMEM((rows, CLUSTER), f32),
            pltpu.VMEM((zone.count, rows, CLUSTER), f32),
            pltpu.VMEM((STEPS, 2 * zone.count, rows, CLUSTER), f32),
            pltpu.VMEM((16, slots), f32),
            pltpu.VMEM((clusters, 3, CLUSTER, CLUSTER), f32),
            pltpu.VMEM((clusters, 16, 2 * CLUSTER), bf16),
            pltpu.VMEM((UNROLL, 2, CLUSTER, CLUSTER), bf16),
            pltpu.VMEM((3, pair_count, CLUSTER), f32),
            pltpu.VMEM((4, pair_count, CLUSTER), f32),
            pltpu.VMEM((zone.count * 8, pair_count), bf16),
            pltpu.VMEM((8, pair_count), bf16),
            pltpu.SemaphoreType.DMA((2 * STEPS, 2 * zone.count)),
            pltpu.SemaphoreType.DMA((2 * STEPS, 2 * zone.count)),
        ],
        compiler_params=pltpu.CompilerParams(collective_id=0, has_side_effects=True),
        name="leapfrog",
    )(pairs, pairs, x, v, q, atoms)
    return tuple(out.reshape(positions.shape) for out in outs)


def solution(mesh):
    spec3 = P(None, "gx", "gy", "gz", None)
    spec1 = P("gx", "gy", "gz", None)
    sizes = tuple(mesh.shape[axis] for axis in AXES)
    return jax.shard_map(
        functools.partial(shards, sizes),
        mesh=mesh,
        in_specs=(spec3, spec3, spec1, spec1, spec3),
        out_specs=(spec3, spec3, spec3),
        check_vma=False,
    )
```

profile of v0, /device:TPU:1, one launch (start us, length us, event | category | flops | bytes accessed | tf_op | source)
XLA Modules:
  0.0 182.4 jit_solution(5793907356004363268)
XLA Ops:
  0.6 179.1 %leapfrog.1 = (f32[3,1,512]{2,1,0:T(1,128)}, f32[3,1,512]{2,1,0:T(1,128)}, f32[3,1,512]{2,1,0:T(1,128)}) custom-call(s32[3,1,256]{2,1,0:T(1,128)} %bitcast.14, s32[3,1,256]{2,1,0:T(1,128)} %bitcast.15, f32[3,1,512]{2,1,0:T(1,128)} %bitcast.19, f32[3,1,512]{2,1,0:T(1,128)} %bitcast.20, f32[1,512]{1,0:T(1,128)} %bitcast.22, s32[1,768]{1,0:T(1,128)} %bitcast.21), custom_call_target="tpu_custom_call" | custom-call | tf_op jit(solution)/shard_map/leapfrog/pallas_call | solution.py:420
  179.7 0.0 copy-start.2
  179.7 0.7 copy-done.2
  180.4 0.0 copy-start.1
  180.4 0.6 copy.14
  181.0 0.1 copy-done.1
  181.1 0.0 copy-start
  181.1 0.6 copy.15
  181.7 0.1 copy-done
  181.8 0.6 copy.16
Async XLA Ops:
  179.7 0.7 copy-start.2
  180.4 0.7 copy-start.1
  181.1 0.7 copy-start
where the time goes:
time: 183 us; the launch traced here: 182 us
  Pallas kernels  179 us (98%)
  local copies, waits for them, and re-layouts  2.67 us (1%)
    pallas_call x1, Pallas kernels, shards(): pl.pallas_call(functools.partial(kernel, zone), out_shape=(shape, shape,...  179 us

commit v1 on v0

v1 whole, which is shorter than its diff:
```python
import functools

import jax
import jax.numpy as jnp
from jax import lax
from jax.experimental import pallas as pl
from jax.experimental.pallas import tpu as pltpu
from jax.sharding import PartitionSpec as P

f32, bf16, i32 = jnp.float32, jnp.bfloat16, jnp.int32
MESH = pl.DeviceIdType.MESH
AXES = ("gx", "gy", "gz")
CLUSTER = 128
CLUSTERS = 6
ATOMS = 512
STEPS = 2
TIME_STEP = 0.02
NB = 10
KR = 32
SR = 48
SLOTS = 384
PLACE = (2, 3, 0, 1, 2)
SIDE = (0, 1, 3, 4)


def split2(v):
    hi = v.astype(bf16).astype(f32)
    return hi, v - hi

def split3f(v):
    a = v.astype(bf16).astype(f32)
    r = v - a
    b = r.astype(bf16).astype(f32)
    return a, b, r - b

def shifted(block, shift):
    return [block[c] + shift[c] if shift[c] is not None else block[c] for c in range(3)]

def weight_rows(coords, charge):
    q = 0.125 * charge
    parts = [split2(q * c) for c in coords] + [split2(q)]
    return [a for a, _ in parts] + [b for _, b in parts]

def put_rows(t_ref, rows, base):
    for n, r in enumerate(rows):
        t_ref[pl.ds(base + n, 8, stride=SR), :] = r

def build_v(t_ref, v_ref, wv_ref, coords, charge, base):
    half = [0.5 * c for c in coords]
    rows = []
    for h in half:
        a, b, c = split3f(h)
        rows += [a, b, a, b, c, a]
    rows += list(split3f(-(half[0]*half[0] + half[1]*half[1] + half[2]*half[2])))
    one = jnp.ones_like(charge)
    rows += [one, one, one]
    put_rows(t_ref, rows, 0)
    put_rows(t_ref, weight_rows(coords, charge), KR)
    for k in range(6):
        v_ref[base + k] = t_ref[k*SR:k*SR+KR, :].astype(bf16)
        wv_ref[base + k] = t_ref[k*SR+KR:(k+1)*SR, :].astype(bf16)

def build_u(t_ref, u_ref, wu_ref, coords, charge, base):
    half = [0.5 * c for c in coords]
    rows = []
    for h in half:
        a, b, c = split3f(h)
        a, b, c = 2.0*a, 2.0*b, 2.0*c
        rows += [a, a, b, b, a, c]
    one = jnp.ones_like(charge)
    rows += [one, one, one]
    rows += list(split3f(1.0 - (half[0]*half[0] + half[1]*half[1] + half[2]*half[2])))
    put_rows(t_ref, rows, 0)
    put_rows(t_ref, weight_rows(coords, charge), KR)
    for k in range(6):
        u_ref[base + k] = jnp.transpose(t_ref[k*SR:k*SR+KR, :]).astype(bf16)
        wu_ref[base + k] = t_ref[k*SR+KR:(k+1)*SR, :].astype(bf16)

def pair_block(code_ref, u_ref, v_ref, wu_ref, wv_ref, f_ref, rawl_ref, rawr_ref):
    def idx(n):
        ui, vi = code_ref[n >> 7, n & 127], code_ref[3 + (n >> 7), n & 127]
        return jnp.clip(ui, 0, u_ref.shape[0] - 1), jnp.clip(vi, 0, v_ref.shape[0] - 1)

    def geometry(slot, n):
        ui, vi = idx(n)
        g0 = jnp.dot(u_ref[ui], v_ref[vi], preferred_element_type=f32)
        g = jnp.maximum(g0, 0.0)
        den = 1.125 - g0
        s = pl.reciprocal(den, approx=True)
        t = (g * s) * (2.0 - den * s)
        f = (g * t) * (t + 3.0)
        hi = f.astype(bf16)
        f_ref[slot, :, 0:128] = hi
        f_ref[slot, :, 128:256] = (f - hi.astype(f32)).astype(bf16)

    def sums(slot, n):
        ui, vi = idx(n)
        fv = f_ref[slot]
        wv = wv_ref[vi]
        left = lax.dot_general(jnp.concatenate([wv, wv], axis=1), fv, (((1,), (1,)), ((), ())),
                               preferred_element_type=f32)
        right = jnp.dot(wu_ref[ui], fv, preferred_element_type=f32)
        return left[0:8], right[0:8, 0:128] + right[0:8, 128:256]

    def keep(n, lr):
        rawl_ref[pl.ds(n, 8, stride=SLOTS), :] = lr[0]
        rawr_ref[pl.ds(n, 8, stride=SLOTS), :] = lr[1]

    return geometry, sums, keep

def block_start(b):
    return (b // 5) * 64 + (b % 5) * 10

def all_pairs(geometry, sums, keep):
    for n in range(NB):
        geometry(n, block_start(0) + n)

    def step(prev, now):
        found = []
        for n in range(NB):
            found.append(sums(n, prev(n)))
            geometry(n, now(n))
            if n > 1:
                keep(prev(n - 2), found[n - 2])
        keep(prev(NB - 2), found[NB - 2])
        keep(prev(NB - 1), found[NB - 1])

    def at(b):
        def f(n):
            e = jnp.maximum((b - 25) * NB + n, 0)
            return jnp.where(b < 25, block_start(jnp.minimum(b, 24)) + n, (e // 6) * 64 + 50 + e % 6)
        return f

    def body(b, c):
        step(at(b - 1), at(b))
        return c
    lax.fori_loop(1, 28, body, 0)
    last = at(27)
    for n in range(NB):
        keep(last(n), sums(n, last(n)))

def reduced(raw_ref, hot_ref):
    cols_hi, cols_lo = [], []
    for c in range(4):
        v = raw_ref[c*SLOTS:(c+1)*SLOTS, :] + raw_ref[(c+4)*SLOTS:(c+5)*SLOTS, :]
        hi = v.astype(bf16)
        cols_hi.append(hi)
        cols_lo.append((v - hi.astype(f32)).astype(bf16))
    rhs = jnp.concatenate([jnp.concatenate(cols_hi, axis=1), jnp.concatenate(cols_lo, axis=1)], axis=0)
    return jnp.dot(hot_ref[...], rhs, preferred_element_type=f32)

def make_hot(code_rows, rows):
    out = []
    for r in code_rows:
        it = lax.broadcasted_iota(i32, (rows, 128), 0)
        out.append(jnp.where(it == r, 1.0, 0.0).astype(bf16))
    one = jnp.concatenate(out, axis=1)
    return jnp.concatenate([one, one], axis=1)


def tables(plate, tower, t_ref, u_ref, v_ref, wu_ref, wv_ref):
    for q in range(5):
        blk = tower(q)
        sh = (None, float(2 - q) if q != 2 else None, None)
        build_u(t_ref, u_ref, wu_ref, shifted(blk, sh), blk[3], q * 6)
    for p in range(5):
        for r in range(5):
            blk = plate(p, PLACE[r])
            sh = (float(p - 2) if p != 2 else None, None, float(r - 2) if r != 2 else None)
            build_v(t_ref, v_ref, wv_ref, shifted(blk, sh), blk[3], (p * 5 + r) * 6)

def finish(plate, tower, out_r, out_l, fr_ref, fl_ref):
    for p in range(5):
        held = {}
        for r in range(5):
            blk = plate(p, PLACE[r])
            sh = (float(p - 2) if p != 2 else None, None, float(r - 2) if r != 2 else None)
            x = shifted(blk, sh)
            rows = slice((p*5+r)*8, (p*5+r)*8+8)
            s = out_r[rows, 384:512]
            fc = [blk[3] * (x[c] * s - out_r[rows, c*128:(c+1)*128]) for c in range(3)]
            z = PLACE[r]
            held[z] = fc if z not in held else [a + b for a, b in zip(held[z], fc)]
        for z in range(4):
            for c in range(3):
                fr_ref[p, z, c] = held[z][c]
    for q in range(5):
        blk = tower(q)
        sh = (None, float(2 - q) if q != 2 else None, None)
        x = shifted(blk, sh)
        s = out_l[q*8:q*8+8, 384:512]
        for c in range(3):
            fl_ref[q, c] = blk[3] * (x[c] * s - out_l[q*8:q*8+8, c*128:(c+1)*128])


def split3(value):
    hi = value.astype(bf16)
    rest = value - hi.astype(f32)
    mid = rest.astype(bf16)
    lo = (rest - mid.astype(f32)).astype(bf16)
    return hi, mid, lo


def one_hot(atoms_ref):
    slots = atoms_ref.shape[1]
    rows = lax.broadcasted_iota(i32, (ATOMS, slots), 0)
    return jnp.where(rows == atoms_ref[...], 1.0, 0.0).astype(bf16)


def sort_pairs(pairs_ref, code_ref):
    count = pairs_ref.shape[2]
    left, right, t = pairs_ref[0], pairs_ref[1], pairs_ref[2]
    t25 = (t * 5243) >> 17
    t5 = (t * 205) >> 10
    q_row = (t5 - 5 * t25).astype(f32)
    pr_row = (t25 * 5 + t - 5 * t5).astype(f32)
    t_row = t.astype(f32)
    rows = jnp.concatenate([t_row, q_row, pr_row, jnp.zeros((125, count), f32)], axis=0)
    cols = jnp.concatenate(
        [jnp.transpose(rows[:, h * 128:(h + 1) * 128]) for h in range(count // 128)], axis=0)
    t_col, q_col, pr_col = cols[:, 0:1], cols[:, 1:2], cols[:, 2:3]
    a = lax.broadcasted_iota(i32, (count, count), 0)
    b = lax.broadcasted_iota(i32, (count, count), 1)
    same = jnp.where(t_col == t_row, 1.0, 0.0)
    earlier = jnp.where(b < a, 1.0, 0.0)
    rank_row = jnp.sum(same * jnp.where(a < b, 1.0, 0.0), axis=0, keepdims=True)
    rank_col = jnp.sum(same * earlier, axis=1, keepdims=True)
    extra_row = jnp.where(rank_row > 1.5, 1.0, 0.0)
    extra_col = jnp.sum(jnp.where(q_col == q_row, earlier * extra_row, 0.0), axis=1, keepdims=True)
    odd = jnp.where((q_col == 1.0) | (q_col == 3.0), 64.0, 0.0)
    place = jnp.where(rank_col < 1.5, 2.0 * pr_col + rank_col, 50.0 + extra_col)
    place = place + odd + 128.0 * q_col
    lane = lax.broadcasted_iota(i32, (count, 640), 1).astype(f32)
    hot = jnp.where(place == lane, 1.0, 0.0).astype(bf16)
    values = jnp.concatenate(
        [left.astype(f32) + 1.0, right.astype(f32) + 1.0, pr_row, jnp.zeros((13, count), f32)],
        axis=0).astype(bf16)
    out = jnp.dot(values, hot, preferred_element_type=f32)
    for q in range(5):
        code_ref[q] = out[0:8, q * 128:(q + 1) * 128].astype(i32)


def decode(blocks, code_vec_ref):
    left_rows, right_rows = [], []
    high = lax.broadcasted_iota(i32, (1, 128), 1) >= 64
    for h in range(3):
        blk = blocks(2 * h)
        if h < 2:
            blk = blk + blocks(2 * h + 1)
        i, j, pr = blk[0:1] - 1, blk[1:2] - 1, blk[2:3]
        q = 2 * h + (jnp.where(high, 1, 0) if h < 2 else jnp.zeros((1, 128), i32))
        code_vec_ref[h:h + 1, :] = q * CLUSTERS + jnp.maximum(i, 0)
        code_vec_ref[3 + h:4 + h, :] = pr * CLUSTERS + jnp.maximum(j, 0)
        left_rows.append(jnp.where(i < 0, -1, q * 8 + i))
        right_rows.append(jnp.where(j < 0, -1, pr * 8 + j))
    code_vec_ref[6:8, :] = jnp.zeros((2, 128), i32)
    return left_rows, right_rows


def kernel(sizes, pairs_ref, x_in, v_in, q_in, atoms_ref, x_out, v_out, f_out,
           plate_ref, tower_ref, vel_ref, fr_ref, fl_ref, landx_ref, landt_ref, landz_ref,
           zsum_ref, code_out_ref, code_in_ref, code_vec_ref, code_ref, slot_ref,
           t_ref, u_ref, v_ref, wu_ref, wv_ref, f_ref, rawl_ref, rawr_ref, hr_ref, hl_ref,
           local_sem, send_sem, recv_sem):
    me = tuple(lax.axis_index(axis) for axis in AXES)

    def peer(axis, offset):
        n = sizes[axis]
        ids = list(me)
        ids[axis] = lax.rem(me[axis] + (offset + n), n)
        return tuple(ids)

    barrier = pltpu.get_barrier_semaphore()
    partners = [(0, d) for d in (-2, -1, 1, 2)] + [(1, d) for d in (-2, -1, 1, 2)]
    partners += [(2, d) for d in (1, 2, 3)]
    for axis, d in partners:
        pl.semaphore_signal(barrier, 1, device_id=peer(axis, d), device_id_type=MESH)

    def copy(step, k, src, dst, to):
        return pltpu.make_async_remote_copy(
            src_ref=src, dst_ref=dst, send_sem=send_sem.at[step, k],
            recv_sem=recv_sem.at[step, k], device_id=to, device_id_type=MESH)

    def comps(step):
        return pl.ds(0, 4) if step == 0 else pl.ds(0, 3)

    def share_z(step, z):
        return copy(step, z - 1, plate_ref.at[step, 2, 0, comps(step)],
                    plate_ref.at[step, 2, z, comps(step)], peer(2, 4 - z))

    def share_t(step, q):
        return copy(step, 3 + SIDE.index(q), plate_ref.at[step, 2, 0, comps(step)],
                    tower_ref.at[step, q, comps(step)], peer(1, q - 2))

    def share_p(step, p, z):
        return copy(step, 7 + SIDE.index(p) * 4 + z, plate_ref.at[step, 2, z, comps(step)],
                    plate_ref.at[step, p, z, comps(step)], peer(0, 2 - p))

    def give_x(step, p):
        return copy(step, 23 + SIDE.index(p), fr_ref.at[step, p], landx_ref.at[step, p],
                    peer(0, p - 2))

    def give_t(step, q):
        return copy(step, 27 + SIDE.index(q), fl_ref.at[step, q], landt_ref.at[step, q],
                    peer(1, 2 - q))

    def give_z(step, z):
        return copy(step, 30 + z, zsum_ref.at[step, z], landz_ref.at[step, z], peer(2, z))

    def share_code(q):
        return copy(0, 34 + SIDE.index(q), code_out_ref.at[q], code_in_ref.at[q], peer(1, q - 2))

    data = jnp.concatenate(
        [x_in[c] for c in range(3)] + [q_in[...]] + [v_in[c] for c in range(3)]
        + [jnp.zeros((1, ATOMS), f32)], axis=0)
    hi, mid, lo = split3(data)
    stacked = jnp.concatenate([hi, mid, lo, jnp.zeros_like(hi)], axis=0)
    out = jnp.dot(stacked, one_hot(atoms_ref), preferred_element_type=f32)
    slot = out[0:8] + out[8:16] + out[16:24]
    vel_ref[...] = jnp.zeros_like(vel_ref)
    plate_ref[0, 2, 0] = jnp.zeros((4, 8, 128), f32)
    for k in range(CLUSTERS):
        lanes = slice(k * CLUSTER, (k + 1) * CLUSTER)
        for c in range(4):
            plate_ref[0, 2, 0, c, pl.ds(k, 1), :] = slot[c:c + 1, lanes]
        for c in range(3):
            vel_ref[c, pl.ds(k, 1), :] = slot[4 + c:5 + c, lanes]
    pl.semaphore_wait(barrier, len(partners))

    def start_share(step):
        for z in (2, 1, 3):
            share_z(step, z).start()
        for q in (0, 4, 1, 3):
            share_t(step, q).start()
        for p in SIDE:
            share_p(step, p, 0).start()

    def forward(step):
        for z in (1, 3, 2):
            share_z(step, z).wait_recv()
            for p in SIDE:
                share_p(step, p, z).start()

    def end_share(step):
        for q in SIDE:
            share_t(step, q).wait_recv()
        for z in (0, 1, 3, 2):
            for p in SIDE:
                share_p(step, p, z).wait_recv()

    start_share(0)
    sort_pairs(pairs_ref, code_out_ref)
    for q in SIDE:
        share_code(q).start()
    rawl_ref[...] = jnp.zeros_like(rawl_ref)
    rawr_ref[...] = jnp.zeros_like(rawr_ref)
    t_ref[...] = jnp.zeros_like(t_ref)
    forward(0)
    for q in SIDE:
        share_code(q).wait_recv()
    left_rows, right_rows = decode(
        lambda q: code_out_ref[q] if q == 2 else code_in_ref[q], code_vec_ref)
    to_smem = pltpu.make_async_copy(code_vec_ref, code_ref, local_sem)
    to_smem.start()
    hl_ref[...] = make_hot(left_rows, 40)
    hr_ref[...] = make_hot(right_rows, 200)
    to_smem.wait()

    geometry, sums, keep = pair_block(
        code_ref, u_ref, v_ref, wu_ref, wv_ref, f_ref, rawl_ref, rawr_ref)

    for step in range(STEPS):
        def plate(p, z):
            return ([plate_ref[step, p, z, c] for c in range(3)] + [plate_ref[0, p, z, 3]])

        def tower(q):
            if q == 2:
                return plate(2, 0)
            return [tower_ref[step, q, c] for c in range(3)] + [tower_ref[0, q, 3]]

        if step > 0:
            forward(step)
        end_share(step)
        tables(plate, tower, t_ref, u_ref, v_ref, wu_ref, wv_ref)
        all_pairs(geometry, sums, keep)
        out_r = reduced(rawr_ref, hr_ref)
        out_l = reduced(rawl_ref, hl_ref)
        finish(plate, tower, out_r, out_l, fr_ref.at[step], fl_ref.at[step])
        for p in SIDE:
            give_x(step, p).start()
        for q in SIDE:
            give_t(step, q).start()
        total = [[fr_ref[step, 2, z, c] for c in range(3)] for z in range(4)]
        for p in SIDE:
            give_x(step, p).wait_recv()
            for z in range(4):
                total[z] = [total[z][c] + landx_ref[step, p, z, c] for c in range(3)]
        for z in (2, 1, 3):
            for c in range(3):
                zsum_ref[step, z, c] = total[z][c]
            give_z(step, z).start()
        force = [total[0][c] + fl_ref[step, 2, c] for c in range(3)]
        for q in SIDE:
            give_t(step, q).wait_recv()
            force = [force[c] + landt_ref[step, q, c] for c in range(3)]
        for z in (1, 3, 2):
            give_z(step, z).wait_recv()
            force = [force[c] + landz_ref[step, z, c] for c in range(3)]
        velocity = [vel_ref[c] + TIME_STEP * force[c] for c in range(3)]
        coords = [plate_ref[step, 2, 0, c] + TIME_STEP * velocity[c] for c in range(3)]
        if step < STEPS - 1:
            for c in range(3):
                plate_ref[step + 1, 2, 0, c] = coords[c]
            start_share(step + 1)
            for c in range(3):
                vel_ref[c] = velocity[c]

    slot_ref[...] = jnp.zeros_like(slot_ref)
    for k in range(CLUSTERS):
        lanes = slice(k * CLUSTER, (k + 1) * CLUSTER)
        for c in range(3):
            slot_ref[pl.ds(c, 1), lanes] = coords[c][k:k + 1]
            slot_ref[pl.ds(3 + c, 1), lanes] = velocity[c][k:k + 1]
            slot_ref[pl.ds(6 + c, 1), lanes] = force[c][k:k + 1]
    stacked = jnp.concatenate(split3(slot_ref[...]), axis=0)
    out = lax.dot_general(
        stacked, one_hot(atoms_ref), (((1,), (1,)), ((), ())), preferred_element_type=f32)
    atom = out[0:16] + out[16:32] + out[32:48]
    for c in range(3):
        x_out[c] = atom[c:c + 1]
        v_out[c] = atom[3 + c:4 + c]
        f_out[c] = atom[6 + c:7 + c]

    for step in range(STEPS):
        for z in (1, 2, 3):
            share_z(step, z).wait_send()
            give_z(step, z).wait_send()
        for s in SIDE:
            share_t(step, s).wait_send()
            give_x(step, s).wait_send()
            give_t(step, s).wait_send()
            for z in range(4):
                share_p(step, s, z).wait_send()
    for q in SIDE:
        share_code(q).wait_send()


def shards(sizes, positions, velocities, charges, cluster_atoms, pair_list):
    slots = cluster_atoms.shape[-1]
    x = positions.reshape(3, 1, ATOMS)
    v = velocities.reshape(3, 1, ATOMS)
    q = charges.reshape(1, ATOMS)
    atoms = cluster_atoms.reshape(1, slots)
    pairs = pair_list.reshape(3, 1, pair_list.shape[-1])
    shape = jax.ShapeDtypeStruct((3, 1, ATOMS), f32)
    vmem = pl.BlockSpec(memory_space=pltpu.VMEM)
    outs = pl.pallas_call(
        functools.partial(kernel, sizes),
        out_shape=(shape, shape, shape),
        in_specs=[vmem] * 5,
        out_specs=(vmem, vmem, vmem),
        scratch_shapes=[
            pltpu.VMEM((STEPS, 5, 4, 4, 8, 128), f32),
            pltpu.VMEM((STEPS, 5, 4, 8, 128), f32),
            pltpu.VMEM((3, 8, 128), f32),
            pltpu.VMEM((STEPS, 5, 4, 3, 8, 128), f32),
            pltpu.VMEM((STEPS, 5, 3, 8, 128), f32),
            pltpu.VMEM((STEPS, 5, 4, 3, 8, 128), f32),
            pltpu.VMEM((STEPS, 5, 3, 8, 128), f32),
            pltpu.VMEM((STEPS, 4, 3, 8, 128), f32),
            pltpu.VMEM((STEPS, 4, 3, 8, 128), f32),
            pltpu.VMEM((5, 8, 128), i32),
            pltpu.VMEM((5, 8, 128), i32),
            pltpu.VMEM((8, 128), i32),
            pltpu.SMEM((8, 128), i32),
            pltpu.VMEM((16, slots), f32),
            pltpu.VMEM((9 * SR, 128), f32),
            pltpu.VMEM((30, 128, KR), bf16),
            pltpu.VMEM((150, KR, 128), bf16),
            pltpu.VMEM((30, 16, 128), bf16),
            pltpu.VMEM((150, 16, 128), bf16),
            pltpu.VMEM((NB, 128, 256), bf16),
            pltpu.VMEM((9 * SLOTS, 128), f32),
            pltpu.VMEM((9 * SLOTS, 128), f32),
            pltpu.VMEM((200, 2 * SLOTS), bf16),
            pltpu.VMEM((40, 2 * SLOTS), bf16),
            pltpu.SemaphoreType.DMA,
            pltpu.SemaphoreType.DMA((STEPS, 38)),
            pltpu.SemaphoreType.DMA((STEPS, 38)),
        ],
        compiler_params=pltpu.CompilerParams(collective_id=0, has_side_effects=True),
        name="leapfrog",
    )(pairs, x, v, q, atoms)
    return tuple(out.reshape(positions.shape) for out in outs)


def solution(mesh):
    spec3 = P(None, "gx", "gy", "gz", None)
    spec1 = P("gx", "gy", "gz", None)
    sizes = tuple(mesh.shape[axis] for axis in AXES)
    return jax.shard_map(
        functools.partial(shards, sizes),
        mesh=mesh,
        in_specs=(spec3, spec3, spec1, spec1, spec3),
        out_specs=(spec3, spec3, spec3),
        check_vma=False,
    )
```

time: 183 us -> 86.5 us (0.47)
  Pallas kernels: 179 us -> 82.9 us
    pallas_call x1, Pallas kernels: 179 us -> 82.9 us  [shards(): pl.pallas_call(functools.partial(kernel, sizes), out_shape=(shape, shape,...]
where the time goes in v1:
time: 86.5 us; the launch traced here: 86.2 us
  Pallas kernels  82.9 us (96%)
  local copies, waits for them, and re-layouts  2.67 us (3%)
    pallas_call x1, Pallas kernels, shards(): pl.pallas_call(functools.partial(kernel, sizes), out_shape=(shape, shape,...  82.9 us
    unnamed x9, local copies, waits for them, and re-layouts  2.67 us

profile of v1, /device:TPU:1, one launch (start us, length us, event | category | flops | bytes accessed | tf_op | source)
XLA Modules:
  0.0 86.2 jit_solution(12167055673727851742)
XLA Ops:
  0.6 82.9 %leapfrog.1 = (f32[3,1,512]{2,1,0:T(1,128)}, f32[3,1,512]{2,1,0:T(1,128)}, f32[3,1,512]{2,1,0:T(1,128)}) custom-call(s32[3,1,256]{2,1,0:T(1,128)} %bitcast.19, f32[3,1,512]{2,1,0:T(1,128)} %bitcast.17, f32[3,1,512]{2,1,0:T(1,128)} %bitcast.18, f32[1,512]{1,0:T(1,128)} %bitcast.21, s32[1,768]{1,0:T(1,128)} %bitcast.20), custom_call_target="tpu_custom_call" | custom-call | tf_op jit(solution)/shard_map/leapfrog/pallas_call | solution.py:457
  83.5 0.0 copy-start.2
  83.5 0.7 copy-done.2
  84.2 0.0 copy-start.1
  84.2 0.6 copy.14
  84.8 0.1 copy-done.1
  84.9 0.0 copy-start
  84.9 0.6 copy.15
  85.5 0.1 copy-done
  85.6 0.6 copy.16
Async XLA Ops:
  83.5 0.7 copy-start.2
  84.2 0.7 copy-start.1
  84.9 0.7 copy-start

commit v2 on v1

v2 whole, which is shorter than its diff:
```python
import functools

import jax
import jax.numpy as jnp
from jax import lax
from jax.experimental import pallas as pl
from jax.experimental.pallas import tpu as pltpu
from jax.sharding import PartitionSpec as P

f32, bf16, i32 = jnp.float32, jnp.bfloat16, jnp.int32
MESH = pl.DeviceIdType.MESH
AXES = ("gx", "gy", "gz")
CLUSTER = 128
CLUSTERS = 6
ATOMS = 512
STEPS = 2
TIME_STEP = 0.02
NB = 8
KR = 32
SR = 48
SLOTS = 384
PLACE = (2, 3, 0, 1, 2)
SIDE = (0, 1, 3, 4)
POSITIONS = (0, 1, 2, 0, 1, 2, 0, 1, 2, 0, 1, 2, 0, 1, 2, 3, 3, 3, 3, 3, 4, 4, 4, 4, 4, 0, 1, 2, 3, 4, 3, 4, 0, 1, 2)
GROUPS = (0, 0, 0, 2, 2, 2, 3, 3, 3, 4, 4, 4, 5, 5, 5, 0, 2, 3, 4, 5, 0, 2, 3, 4, 5, 6, 6, 6, 6, 6, 1, 1, 1, 1, 1)


def split2(v):
    hi = v.astype(bf16).astype(f32)
    return hi, v - hi


def split3f(v):
    a = v.astype(bf16).astype(f32)
    r = v - a
    b = r.astype(bf16).astype(f32)
    return a, b, r - b


def weight_rows(coords, charge):
    q = 0.125 * charge
    parts = [split2(q * c) for c in coords] + [split2(q)]
    return [a for a, _ in parts] + [b for _, b in parts]


def put_rows(t_ref, rows, base):
    for n, r in enumerate(rows):
        t_ref[pl.ds(base + n, 8, stride=SR), :] = r


def half_square(half):
    return half[0] * half[0] + half[1] * half[1] + half[2] * half[2]


def build_v(t_ref, v_ref, wv_ref, coords, charge, base):
    half = [0.5 * c for c in coords]
    rows = []
    for h in half:
        a, b, c = split3f(h)
        rows += [a, b, a, b, c, a]
    rows += list(split3f(-half_square(half)))
    one = jnp.ones_like(charge)
    rows += [one, one, one]
    put_rows(t_ref, rows, 0)
    put_rows(t_ref, weight_rows(coords, charge), KR + 8)
    for k in range(CLUSTERS):
        v_ref[base + k] = t_ref[k * SR:k * SR + KR, :].astype(bf16)
        wv_ref[base + k] = t_ref[k * SR + KR:(k + 1) * SR, :].astype(bf16)


def build_u(t_ref, u_ref, wu_ref, coords, charge, base):
    half = [0.5 * c for c in coords]
    rows = []
    for h in half:
        a, b, c = split3f(h)
        a, b, c = 2.0 * a, 2.0 * b, 2.0 * c
        rows += [a, a, b, b, a, c]
    one = jnp.ones_like(charge)
    rows += [one, one, one]
    rows += list(split3f(1.0 - half_square(half)))
    put_rows(t_ref, rows, 0)
    put_rows(t_ref, weight_rows(coords, charge), KR)
    for k in range(CLUSTERS):
        u_ref[base + k] = jnp.transpose(t_ref[k * SR:k * SR + KR, :]).astype(bf16)
        wu_ref[base + k] = t_ref[k * SR + KR:(k + 1) * SR, :].astype(bf16)


class Pairs:

    def __init__(self, code_ref, u_ref, v_ref, wu_ref, wv_ref, g_ref, f_ref, rawl_ref, rawr_ref):
        self.code, self.u, self.v, self.wu, self.wv = code_ref, u_ref, v_ref, wu_ref, wv_ref
        self.g, self.f, self.rawl, self.rawr = g_ref, f_ref, rawl_ref, rawr_ref

    def tables(self, place, m):
        q, group = place
        lane = (q & 1) * 64 + group * 8 + m
        ui, vi = self.code[q, 0, lane], self.code[q, 1, lane]
        return jnp.clip(ui, 0, self.u.shape[0] - 1), jnp.clip(vi, 0, self.v.shape[0] - 1)

    def distance(self, place, m, buf):
        ui, vi = self.tables(place, m)
        self.g[buf, m] = jnp.dot(self.u[ui], self.v[vi], preferred_element_type=f32)

    def factor(self, m, buf):
        g0 = self.g[buf, m]
        g = jnp.maximum(g0, 0.0)
        den = 1.125 - g0
        s = pl.reciprocal(den, approx=True)
        t = (g * s) * (2.0 - den * s)
        f = (g * t) * (t + 3.0)
        hi = f.astype(bf16)
        self.f[buf, m, 0] = hi
        self.f[buf, m, 1] = (f - hi.astype(f32)).astype(bf16)

    def sums(self, place, m, buf):
        ui, vi = self.tables(place, m)
        hi, lo = self.f[buf, m, 0], self.f[buf, m, 1]
        both = jnp.concatenate([
            jnp.concatenate([hi, lo], axis=1),
            jnp.concatenate([jnp.transpose(hi), jnp.transpose(lo)], axis=1)], axis=0)
        weights = jnp.concatenate([self.wu[ui], self.wv[vi]], axis=1)
        out = jnp.dot(weights, both, preferred_element_type=f32)
        out = out[:, 0:128] + out[:, 128:256]
        n = place[0] * 64 + place[1] * 8 + m
        self.rawr[pl.ds(n, 8, stride=SLOTS), :] = out[0:8]
        self.rawl[pl.ds(n, 8, stride=SLOTS), :] = out[8:16]

    def stage(self, parity, here, done, factors=True):
        for m in range(NB):
            if done is not None:
                self.sums(done, m, parity)
            if factors:
                self.factor(m, 1 - parity)
            if here is not None:
                self.distance(here, m, parity)


def reduced(raw_ref, hot):
    cols_hi, cols_lo = [], []
    for c in range(4):
        v = raw_ref[c * SLOTS:(c + 1) * SLOTS, :] + raw_ref[(c + 4) * SLOTS:(c + 5) * SLOTS, :]
        hi = v.astype(bf16)
        cols_hi.append(hi)
        cols_lo.append((v - hi.astype(f32)).astype(bf16))
    rhs = jnp.concatenate(
        [jnp.concatenate(cols_hi, axis=1), jnp.concatenate(cols_lo, axis=1)], axis=0)
    return jnp.dot(hot, rhs, preferred_element_type=f32)


def make_hot(code_rows, rows):
    out = []
    for r in code_rows:
        it = lax.broadcasted_iota(i32, (rows, 128), 0)
        out.append(jnp.where(it == r, 1.0, 0.0).astype(bf16))
    one = jnp.concatenate(out, axis=1)
    return jnp.concatenate([one, one], axis=1)


def force_rows(coords, charge, out, row):
    s = out[row:row + 8, 384:512]
    return [charge * (coords[c] * s - out[row:row + 8, c * 128:(c + 1) * 128]) for c in range(3)]


def split3(value):
    hi = value.astype(bf16)
    rest = value - hi.astype(f32)
    mid = rest.astype(bf16)
    lo = (rest - mid.astype(f32)).astype(bf16)
    return hi, mid, lo


def one_hot(atoms_ref):
    slots = atoms_ref.shape[1]
    rows = lax.broadcasted_iota(i32, (ATOMS, slots), 0)
    return jnp.where(rows == atoms_ref[...], 1.0, 0.0).astype(bf16)


def sort_pairs(pairs_ref, code_ref):
    count = pairs_ref.shape[2]
    left, right, t = pairs_ref[0], pairs_ref[1], pairs_ref[2]
    t25 = (t * 5243) >> 17
    t5 = (t * 205) >> 10
    q_row = (t5 - 5 * t25).astype(f32)
    pr_row = (t25 * 5 + t - 5 * t5).astype(f32)
    t_row = t.astype(f32)
    rows = jnp.concatenate([t_row, q_row, pr_row, jnp.zeros((125, count), f32)], axis=0)
    cols = jnp.concatenate(
        [jnp.transpose(rows[:, h * 128:(h + 1) * 128]) for h in range(count // 128)], axis=0)
    t_col, q_col, pr_col = cols[:, 0:1], cols[:, 1:2], cols[:, 2:3]
    a = lax.broadcasted_iota(i32, (count, count), 0)
    b = lax.broadcasted_iota(i32, (count, count), 1)
    same = jnp.where(t_col == t_row, 1.0, 0.0)
    earlier = jnp.where(b < a, 1.0, 0.0)
    rank_row = jnp.sum(same * jnp.where(a < b, 1.0, 0.0), axis=0, keepdims=True)
    rank_col = jnp.sum(same * earlier, axis=1, keepdims=True)
    extra_row = jnp.where(rank_row > 1.5, 1.0, 0.0)
    extra_col = jnp.sum(jnp.where(q_col == q_row, earlier * extra_row, 0.0), axis=1, keepdims=True)
    odd = jnp.where((q_col == 1.0) | (q_col == 3.0), 64.0, 0.0)
    p_col = jnp.floor((pr_col + 0.5) * 0.2)
    r_col = pr_col - 5.0 * p_col
    pi = jnp.where(p_col > 2.0, p_col - 1.0, p_col)
    ri = jnp.where(r_col == 1.0, 0.0, jnp.where(r_col == 3.0, 1.0, jnp.where(r_col == 0.0, 2.0, 3.0)))
    group = jnp.where(p_col == 2.0, 8.0 + 2.0 * ri, 16.0 + 8.0 * ri + 2.0 * pi)
    group = jnp.where(r_col == 2.0, jnp.where(p_col == 2.0, 48.0, 2.0 * pi), group)
    place = jnp.where(rank_col < 1.5, group + rank_col, 50.0 + extra_col)
    place = place + odd + 128.0 * q_col
    lane = lax.broadcasted_iota(i32, (count, 640), 1).astype(f32)
    hot = jnp.where(place == lane, 1.0, 0.0).astype(bf16)
    values = jnp.concatenate(
        [left.astype(f32) + 1.0, right.astype(f32) + 1.0, pr_row, jnp.zeros((13, count), f32)],
        axis=0).astype(bf16)
    out = jnp.dot(values, hot, preferred_element_type=f32)
    for q in range(5):
        code_ref[q] = out[0:8, q * 128:(q + 1) * 128].astype(i32)


def decode(code_in_ref, code_vec_ref, q):
    blk = code_in_ref[q]
    i, j, pr = blk[0:1] - 1, blk[1:2] - 1, blk[2:3]
    code_vec_ref[q, 0:1, :] = q * CLUSTERS + jnp.maximum(i, 0)
    code_vec_ref[q, 1:2, :] = pr * CLUSTERS + jnp.maximum(j, 0)
    code_vec_ref[q, 2:8, :] = jnp.zeros((6, 128), i32)


def sum_rows(code_in_ref):
    left_rows, right_rows = [], []
    high = lax.broadcasted_iota(i32, (1, 128), 1) >= 64
    for h in range(3):
        blk = code_in_ref[2 * h]
        if h < 2:
            blk = blk + code_in_ref[2 * h + 1]
        i, j, pr = blk[0:1] - 1, blk[1:2] - 1, blk[2:3]
        q = 2 * h + (jnp.where(high, 1, 0) if h < 2 else jnp.zeros((1, 128), i32))
        pr = jnp.where(pr < 10, pr, jnp.where(pr < 15, pr + 10, pr - 5))
        left_rows.append(jnp.where(i < 0, -1, q * 8 + i))
        right_rows.append(jnp.where(j < 0, -1, pr * 8 + j))
    return left_rows, right_rows


def kernel(sizes, pairs_hbm, x_hbm, v_hbm, q_hbm, atoms_hbm, x_out, v_out, f_out,
           pairs_ref, x_in, v_in, q_in, atoms_ref,
           plate_ref, tower_ref, vel_ref, fr_ref, fl_ref, landx_ref, landt_ref, landz_ref,
           zsum_ref, code_in_ref, code_send_ref, code_vec_ref, code_ref, slot_ref,
           t_ref, tu_ref, u_ref, v_ref, wu_ref, wv_ref, g_ref, f_ref, rawl_ref, rawr_ref, hr_ref, hl_ref,
           load_sem, local_sem, send_sem, recv_sem):
    me = tuple(lax.axis_index(axis) for axis in AXES)
    column = me[1] & 3
    mirrored = column >= 2
    inner = jnp.where(mirrored, 3 - column, column)

    def tower_at(pos):
        third = jnp.where(inner == 0, 0, 3)
        q = jnp.where(pos == 0, 2, jnp.where(pos == 1, 1, jnp.where(
            pos == 2, third, jnp.where(pos == 3, 3 - third, 4))))
        return jnp.where(mirrored, 4 - q, q)

    def peer(axis, offset):
        n = sizes[axis]
        ids = list(me)
        ids[axis] = lax.rem(me[axis] + (offset + n), n)
        return tuple(ids)

    barrier = pltpu.get_barrier_semaphore()
    partners = [(0, d) for d in (-2, -1, 1, 2)] + [(1, d) for d in (-2, -1, 1, 2)]
    partners += [(2, d) for d in (1, 2, 3)]
    for axis, d in partners:
        pl.semaphore_signal(barrier, 1, device_id=peer(axis, d), device_id_type=MESH)
    loads = [
        pltpu.make_async_copy(src, dst, load_sem.at[n]) for n, (src, dst) in enumerate(
            ((atoms_hbm, atoms_ref), (x_hbm, x_in), (q_hbm, q_in), (v_hbm, v_in), (pairs_hbm, pairs_ref)))]
    for load in loads:
        load.start()

    def copy(step, k, src, dst, to):
        return pltpu.make_async_remote_copy(
            src_ref=src, dst_ref=dst, send_sem=send_sem.at[step, k],
            recv_sem=recv_sem.at[step, k], device_id=to, device_id_type=MESH)

    def comps(step):
        return pl.ds(0, 4) if step == 0 else pl.ds(0, 3)

    def share_z(step, z):
        return copy(step, z, plate_ref.at[step, 2, 0, comps(step)],
                    plate_ref.at[step, 2, z, comps(step)], peer(2, 4 - z))

    def share_t(step, q):
        return copy(step, 4 + q, plate_ref.at[step, 2, 0, comps(step)],
                    tower_ref.at[step, q, comps(step)], peer(1, q - 2))

    def share_p(step, p, z):
        return copy(step, 9 + p * 4 + z, plate_ref.at[step, 2, z, comps(step)],
                    plate_ref.at[step, p, z, comps(step)], peer(0, 2 - p))

    def give_x(step, p, z):
        return copy(step, 29 + p * 4 + z, fr_ref.at[step, p, z], landx_ref.at[step, p, z],
                    peer(0, p - 2))

    def give_t(step, half, q):
        return copy(step, 49 + q, fl_ref.at[step, half, q], landt_ref.at[step, q],
                    peer(1, 2 - q))

    def give_z(step, z):
        return copy(step, 54 + z, zsum_ref.at[step, z], landz_ref.at[step, z], peer(2, z))

    def share_code(q):
        return copy(0, 58 + q, code_send_ref.at[q], code_in_ref.at[q], peer(1, q - 2))

    def to_smem(q):
        return pltpu.make_async_copy(code_vec_ref.at[q], code_ref.at[q], local_sem.at[q])

    with jax.named_scope("slots"):
        plate_ref[0, 2, 0] = jnp.zeros((4, 8, 128), f32)
        vel_ref[...] = jnp.zeros_like(vel_ref)
        rawl_ref[...] = jnp.zeros_like(rawl_ref)
        rawr_ref[...] = jnp.zeros_like(rawr_ref)
        t_ref[...] = jnp.zeros_like(t_ref)
        tu_ref[...] = jnp.zeros_like(tu_ref)
        for load in loads[:4]:
            load.wait()
        data = jnp.concatenate(
            [x_in[c] for c in range(3)] + [q_in[...]] + [v_in[c] for c in range(3)]
            + [jnp.zeros((1, ATOMS), f32)], axis=0)
        hi, mid, lo = split3(data)
        stacked = jnp.concatenate([hi, mid, lo, jnp.zeros_like(hi)], axis=0)
        out = jnp.dot(stacked, one_hot(atoms_ref), preferred_element_type=f32)
        slot = out[0:8] + out[8:16] + out[16:24]
        for k in range(CLUSTERS):
            lanes = slice(k * CLUSTER, (k + 1) * CLUSTER)
            for c in range(4):
                plate_ref[0, 2, 0, c, pl.ds(k, 1), :] = slot[c:c + 1, lanes]
            for c in range(3):
                vel_ref[c, pl.ds(k, 1), :] = slot[4 + c:5 + c, lanes]
    with jax.named_scope("sort"):
        loads[4].wait()
        sort_pairs(pairs_ref, code_send_ref)
        code_in_ref[2] = code_send_ref[2]

    def start_share(step):
        for z in (2, 1, 3):
            share_z(step, z).start()
        for p in SIDE:
            share_p(step, p, 0).start()
        for q in (0, 4, 1, 3):
            share_t(step, q).start()

    with jax.named_scope("barrier"):
        pl.semaphore_wait(barrier, len(partners))
    start_share(0)
    for q in (0, 4, 1, 3):
        share_code(q).start()

    order_of_towers = sum(tower_at(pos) << (3 * pos) for pos in range(5))

    def order(i):
        word = (i * 103) >> 10
        place = 3 * (i - 10 * word)

        def entry(table):
            words = [sum(v << (3 * n) for n, v in enumerate(table[w:w + 10])) for w in range(0, 40, 10)]
            if isinstance(i, int):
                return (words[word] >> place) & 7
            pick = jnp.where(word < 2, jnp.where(word < 1, words[0], words[1]),
                             jnp.where(word < 3, words[2], words[3]))
            return (pick >> place) & 7

        return (order_of_towers >> (3 * entry(POSITIONS))) & 7, entry(GROUPS)

    pairs = Pairs(code_ref, u_ref, v_ref, wu_ref, wv_ref, g_ref, f_ref, rawl_ref, rawr_ref)

    def moved(block, shift):
        return [block[c] if shift[c] is None else block[c] + shift[c] for c in range(3)]

    def plate(step, p, r):
        z = PLACE[r]
        block = [plate_ref[step, p, z, c] for c in range(3)]
        shift = (None if p == 2 else float(p - 2), None, None if r == 2 else float(r - 2))
        return moved(block, shift), plate_ref[0, p, z, 3]

    def tower(step, q):
        if isinstance(q, int) and q == 2:
            return [plate_ref[step, 2, 0, c] for c in range(3)], plate_ref[0, 2, 0, 3]
        shift = (None, jnp.asarray(2 - q, f32), None)
        return moved([tower_ref[step, q, c] for c in range(3)], shift), tower_ref[0, q, 3]

    def v_table(step, p, r):
        coords, charge = plate(step, p, r)
        build_v(t_ref, v_ref, wv_ref, coords, charge, (p * 5 + r) * CLUSTERS)

    def u_table(step, q):
        coords, charge = tower(step, q)
        build_u(tu_ref, u_ref, wu_ref, coords, charge, q * CLUSTERS)

    def tower_in(step, pos):
        q = tower_at(pos)
        share_t(step, q).wait_recv()
        u_table(step, q)

    def codes_in(near):
        for pos in near:
            q = 2 if pos == 0 else tower_at(pos)
            if pos > 0:
                share_code(q).wait_recv()
            decode(code_in_ref, code_vec_ref, q)
            to_smem(q).start()
        for pos in near:
            to_smem(2 if pos == 0 else tower_at(pos)).wait()

    for step in range(STEPS):
        u_table(step, 2)
        v_table(step, 2, 2)
        if step == 0:
            codes_in((0,))
        with jax.named_scope("forward"):
            for z in (1, 3, 2):
                share_z(step, z).wait_recv()
                for p in SIDE:
                    share_p(step, p, z).start()
        with jax.named_scope("near_x"):
            for p in SIDE:
                share_p(step, p, 0).wait_recv()
                v_table(step, p, 2)
        pairs.stage(0, order(0), None, False)
        if step == 0:
            codes_in((1, 2))
        tower_in(step, 1)
        pairs.stage(1, order(1), None)
        tower_in(step, 2)
        pairs.stage(0, order(2), order(0))

        def two_blocks(k, carry):
            i = 3 + 2 * k

            @pl.when(k == 0)
            def _():
                with jax.named_scope("far_x"):
                    for z, r in ((1, 3), (3, 1)):
                        for p in SIDE:
                            share_p(step, p, z).wait_recv()
                            v_table(step, p, r)

            @pl.when(k == 3)
            def _():
                with jax.named_scope("far_x2"):
                    for p in SIDE:
                        share_p(step, p, 2).wait_recv()
                        v_table(step, p, 0)
                        v_table(step, p, 4)
                    for r in SIDE:
                        v_table(step, 2, r)

            @pl.when(k == 6)
            def _():
                with jax.named_scope("tower3"):
                    if step == 0:
                        codes_in((3, 4))
                    tower_in(step, 3)

            @pl.when(k == 8)
            def _():
                with jax.named_scope("tower4"):
                    tower_in(step, 4)

            here, later = order(i), order(i + 1)
            pairs.stage(1, here, carry[0:2])
            pairs.stage(0, later, carry[2:4])
            return here + later

        with jax.named_scope("loop"):
            last = lax.fori_loop(0, 15, two_blocks, tuple(
                jnp.asarray(v, i32) for v in order(1) + order(2)))
        pairs.stage(1, order(33), last[0:2])
        with jax.named_scope("first_sums"):
            if step == 0:
                left_rows, right_rows = sum_rows(code_in_ref)
                hl_ref[...] = make_hot(left_rows, 40)
                hr_ref[...] = make_hot(right_rows, 200)
            out = reduced(rawr_ref, hr_ref[0:160])
            for z, rs in ((2, (0, 4)), (1, (3,)), (3, (1,)), (0, (2,))):
                for n, p in enumerate(SIDE):
                    parts = [force_rows(*plate(step, p, r), out, (n * 5 + r) * 8) for r in rs]
                    for c in range(3):
                        fr_ref[step, p, z, c] = sum(part[c] for part in parts[1:]) + parts[0][c] if (
                            len(parts) > 1) else parts[0][c]
                    give_x(step, p, z).start()
            out = reduced(rawl_ref, hl_ref[...])
            for q in SIDE:
                part = force_rows(*tower(step, q), out, q * 8)
                for c in range(3):
                    fl_ref[step, 0, q, c] = part[c]
            for pos in (4, 3):
                give_t(step, 0, tower_at(pos)).start()
        with jax.named_scope("late"):
            pairs.stage(0, order(34), last[2:4])
            pairs.stage(1, None, order(33))
            pairs.stage(0, None, order(34), False)
        with jax.named_scope("last_sums"):
            out = reduced(rawl_ref, hl_ref[...])
            for q in range(5):
                part = force_rows(*tower(step, q), out, q * 8)
                for c in range(3):
                    fl_ref[step, 1, q, c] = part[c]
            for pos in (2, 1):
                give_t(step, 1, tower_at(pos)).start()
            out = reduced(rawr_ref, hr_ref[160:200])
            parts = [force_rows(*plate(step, 2, r), out, r * 8) for r in range(5)]
        total = {2: [a + b for a, b in zip(parts[0], parts[4])], 1: parts[3], 3: parts[1], 0: parts[2]}
        for z in (2, 1, 3, 0):
            with jax.named_scope("give_x"):
                for p in SIDE:
                    give_x(step, p, z).wait_recv()
            for p in SIDE:
                total[z] = [total[z][c] + landx_ref[step, p, z, c] for c in range(3)]
            if z > 0:
                for c in range(3):
                    zsum_ref[step, z, c] = total[z][c]
                give_z(step, z).start()
        force = [total[0][c] + fl_ref[step, 1, 2, c] for c in range(3)]
        with jax.named_scope("give_t"):
            for q in SIDE:
                give_t(step, 0, q).wait_recv()
        for q in SIDE:
            force = [force[c] + landt_ref[step, q, c] for c in range(3)]
        with jax.named_scope("give_z"):
            for z in (1, 3, 2):
                give_z(step, z).wait_recv()
        for z in (1, 3, 2):
            force = [force[c] + landz_ref[step, z, c] for c in range(3)]
        velocity = [vel_ref[c] + TIME_STEP * force[c] for c in range(3)]
        coords = [plate_ref[step, 2, 0, c] + TIME_STEP * velocity[c] for c in range(3)]
        if step < STEPS - 1:
            for c in range(3):
                plate_ref[step + 1, 2, 0, c] = coords[c]
            start_share(step + 1)
            for c in range(3):
                vel_ref[c] = velocity[c]

    with jax.named_scope("output"):
        slot_ref[...] = jnp.zeros_like(slot_ref)
        for k in range(CLUSTERS):
            lanes = slice(k * CLUSTER, (k + 1) * CLUSTER)
            for c in range(3):
                slot_ref[pl.ds(c, 1), lanes] = coords[c][k:k + 1]
                slot_ref[pl.ds(3 + c, 1), lanes] = velocity[c][k:k + 1]
                slot_ref[pl.ds(6 + c, 1), lanes] = force[c][k:k + 1]
        stacked = jnp.concatenate(split3(slot_ref[...]), axis=0)
        out = lax.dot_general(
            stacked, one_hot(atoms_ref), (((1,), (1,)), ((), ())), preferred_element_type=f32)
        atom = out[0:16] + out[16:32] + out[32:48]
        for c in range(3):
            x_out[c] = atom[c:c + 1]
            v_out[c] = atom[3 + c:4 + c]
            f_out[c] = atom[6 + c:7 + c]

    for step in range(STEPS):
        for z in (1, 2, 3):
            share_z(step, z).wait_send()
            give_z(step, z).wait_send()
        for s in SIDE:
            share_t(step, s).wait_send()
            for z in range(4):
                share_p(step, s, z).wait_send()
                give_x(step, s, z).wait_send()
        for pos in (4, 3):
            give_t(step, 0, tower_at(pos)).wait_send()
        for pos in (2, 1):
            give_t(step, 1, tower_at(pos)).wait_send()
    for q in SIDE:
        share_code(q).wait_send()


def shards(sizes, positions, velocities, charges, cluster_atoms, pair_list):
    slots = cluster_atoms.shape[-1]
    x = positions.reshape(3, 1, ATOMS)
    v = velocities.reshape(3, 1, ATOMS)
    q = charges.reshape(1, ATOMS)
    atoms = cluster_atoms.reshape(1, slots)
    pairs = pair_list.reshape(3, 1, pair_list.shape[-1])
    shape = jax.ShapeDtypeStruct((3, 1, ATOMS), f32)
    vmem = pl.BlockSpec(memory_space=pltpu.VMEM)
    outs = pl.pallas_call(
        functools.partial(kernel, sizes),
        out_shape=(shape, shape, shape),
        in_specs=[pl.BlockSpec(memory_space=pl.ANY)] * 5,
        out_specs=(vmem, vmem, vmem),
        scratch_shapes=[
            pltpu.VMEM(pairs.shape, i32),
            pltpu.VMEM(x.shape, f32),
            pltpu.VMEM(v.shape, f32),
            pltpu.VMEM(q.shape, f32),
            pltpu.VMEM(atoms.shape, i32),
            pltpu.VMEM((STEPS, 5, 4, 4, 8, 128), f32),
            pltpu.VMEM((STEPS, 5, 4, 8, 128), f32),
            pltpu.VMEM((3, 8, 128), f32),
            pltpu.VMEM((STEPS, 5, 4, 3, 8, 128), f32),
            pltpu.VMEM((STEPS, 2, 5, 3, 8, 128), f32),
            pltpu.VMEM((STEPS, 5, 4, 3, 8, 128), f32),
            pltpu.VMEM((STEPS, 5, 3, 8, 128), f32),
            pltpu.VMEM((STEPS, 4, 3, 8, 128), f32),
            pltpu.VMEM((STEPS, 4, 3, 8, 128), f32),
            pltpu.VMEM((5, 8, 128), i32),
            pltpu.VMEM((5, 8, 128), i32),
            pltpu.VMEM((5, 8, 128), i32),
            pltpu.SMEM((5, 8, 128), i32),
            pltpu.VMEM((16, slots), f32),
            pltpu.VMEM((9 * SR, 128), f32),
            pltpu.VMEM((9 * SR, 128), f32),
            pltpu.VMEM((30, 128, KR), bf16),
            pltpu.VMEM((150, KR, 128), bf16),
            pltpu.VMEM((30, 16, 128), bf16),
            pltpu.VMEM((150, 16, 128), bf16),
            pltpu.VMEM((2, NB, 128, 128), f32),
            pltpu.VMEM((2, NB, 2, 128, 128), bf16),
            pltpu.VMEM((9 * SLOTS, 128), f32),
            pltpu.VMEM((9 * SLOTS, 128), f32),
            pltpu.VMEM((200, 2 * SLOTS), bf16),
            pltpu.VMEM((40, 2 * SLOTS), bf16),
            pltpu.SemaphoreType.DMA((5,)),
            pltpu.SemaphoreType.DMA((5,)),
            pltpu.SemaphoreType.DMA((STEPS, 63)),
            pltpu.SemaphoreType.DMA((STEPS, 63)),
        ],
        compiler_params=pltpu.CompilerParams(collective_id=0, has_side_effects=True),
        name="leapfrog",
    )(pairs, x, v, q, atoms)
    return tuple(out.reshape(positions.shape) for out in outs)


def solution(mesh):
    spec3 = P(None, "gx", "gy", "gz", None)
    spec1 = P("gx", "gy", "gz", None)
    sizes = tuple(mesh.shape[axis] for axis in AXES)
    return jax.shard_map(
        functools.partial(shards, sizes),
        mesh=mesh,
        in_specs=(spec3, spec3, spec1, spec1, spec3),
        out_specs=(spec3, spec3, spec3),
        check_vma=False,
    )
```

time: 86.5 us -> 80.2 us (0.927)
  Pallas kernels: 82.9 us -> 76.6 us
    pallas_call x1, Pallas kernels: 82.9 us -> 76.6 us  [shards(): pl.pallas_call(functools.partial(kernel, sizes), out_shape=(shape, shape,...]
where the time goes in v2:
time: 80.2 us; the launch traced here: 79.9 us
  Pallas kernels  76.6 us (96%)
  local copies, waits for them, and re-layouts  2.67 us (3%)
    pallas_call x1, Pallas kernels, shards(): pl.pallas_call(functools.partial(kernel, sizes), out_shape=(shape, shape,...  76.6 us
    unnamed x9, local copies, waits for them, and re-layouts  2.67 us

profile of v2, /device:TPU:1, one launch (start us, length us, event | category | flops | bytes accessed | tf_op | source)
XLA Modules:
  0.0 79.9 jit_solution(8953899429661329618)
XLA Ops:
  0.6 76.6 %leapfrog.1 = (f32[3,1,512]{2,1,0:T(1,128)}, f32[3,1,512]{2,1,0:T(1,128)}, f32[3,1,512]{2,1,0:T(1,128)}) custom-call(s32[3,1,256]{2,1,0:T(1,128)} %bitcast.19, f32[3,1,512]{2,1,0:T(1,128)} %bitcast.17, f32[3,1,512]{2,1,0:T(1,128)} %bitcast.18, f32[1,512]{1,0:T(1,128)} %bitcast.21, s32[1,768]{1,0:T(1,128)} %bitcast.20), custom_call_target="tpu_custom_call" | custom-call | tf_op jit(solution)/shard_map/leapfrog/pallas_call | solution.py:580
  77.2 0.0 copy-start.2
  77.2 0.7 copy-done.2
  77.9 0.0 copy-start.1
  77.9 0.6 copy.14
  78.5 0.1 copy-done.1
  78.6 0.0 copy-start
  78.6 0.6 copy.15
  79.2 0.1 copy-done
  79.3 0.6 copy.16
Async XLA Ops:
  77.2 0.7 copy-start.2
  77.9 0.7 copy-start.1
  78.6 0.7 copy-start

commit v3 on v2

--- a/solution.py
+++ b/solution.py
@@ -121,9 +121,9 @@
         weights = jnp.concatenate([self.wu[ui], self.wv[vi]], axis=1)
         out = jnp.dot(weights, both, preferred_element_type=f32)
         out = out[:, 0:128] + out[:, 128:256]
-        n = place[0] * 64 + place[1] * 8 + m
-        self.rawr[pl.ds(n, 8, stride=SLOTS), :] = out[0:8]
-        self.rawl[pl.ds(n, 8, stride=SLOTS), :] = out[8:16]
+        n = pl.multiple_of(8 * (place[0] * 64 + place[1] * 8 + m), 8)
+        self.rawr[pl.ds(n, 8), :] = out[0:8]
+        self.rawl[pl.ds(n, 8), :] = out[8:16]
 
     def stage(self, parity, here, done, factors=True):
         for m in range(NB):
@@ -138,7 +138,7 @@
 def reduced(raw_ref, hot):
     cols_hi, cols_lo = [], []
     for c in range(4):
-        v = raw_ref[c * SLOTS:(c + 1) * SLOTS, :] + raw_ref[(c + 4) * SLOTS:(c + 5) * SLOTS, :]
+        v = raw_ref[pl.ds(c, SLOTS, stride=8), :] + raw_ref[pl.ds(c + 4, SLOTS, stride=8), :]
         hi = v.astype(bf16)
         cols_hi.append(hi)
         cols_lo.append((v - hi.astype(f32)).astype(bf16))

time: 80.2 us -> 79.2 us (0.988)
  Pallas kernels: 76.6 us -> 75.6 us
    pallas_call x1, Pallas kernels: 76.6 us -> 75.6 us  [shards(): pl.pallas_call(functools.partial(kernel, sizes), out_shape=(shape, shape,...]
where the time goes in v3:
time: 79.2 us; the launch traced here: 79 us
  Pallas kernels  75.6 us (95%)
  local copies, waits for them, and re-layouts  2.67 us (3%)
    pallas_call x1, Pallas kernels, shards(): pl.pallas_call(functools.partial(kernel, sizes), out_shape=(shape, shape,...  75.6 us
    unnamed x9, local copies, waits for them, and re-layouts  2.67 us

profile of v3, /device:TPU:1, one launch (start us, length us, event | category | flops | bytes accessed | tf_op | source)
XLA Modules:
  0.0 79.0 jit_solution(7987127108782997535)
XLA Ops:
  0.6 75.6 %leapfrog.1 = (f32[3,1,512]{2,1,0:T(1,128)}, f32[3,1,512]{2,1,0:T(1,128)}, f32[3,1,512]{2,1,0:T(1,128)}) custom-call(s32[3,1,256]{2,1,0:T(1,128)} %bitcast.19, f32[3,1,512]{2,1,0:T(1,128)} %bitcast.17, f32[3,1,512]{2,1,0:T(1,128)} %bitcast.18, f32[1,512]{1,0:T(1,128)} %bitcast.21, s32[1,768]{1,0:T(1,128)} %bitcast.20), custom_call_target="tpu_custom_call" | custom-call | tf_op jit(solution)/shard_map/leapfrog/pallas_call | solution.py:580
  76.3 0.0 copy-start.2
  76.3 0.7 copy-done.2
  77.0 0.0 copy-start.1
  77.0 0.6 copy.14
  77.6 0.1 copy-done.1
  77.7 0.0 copy-start
  77.7 0.6 copy.15
  78.3 0.1 copy-done
  78.4 0.6 copy.16
Async XLA Ops:
  76.3 0.7 copy-start.2
  77.0 0.7 copy-start.1
  77.7 0.7 copy-start
